TPU v7x, 128 devices: a whole 4x4x4 slice. The times are simulated.
128 devices in a mesh: pa: 8 (over z_lo, y), pb: 16 (over z_hi, x, core).
Axes of the slice: x: 4, y: 4, z: 4 (z_hi: 2, z_lo: 2; z = z_hi * 2 + z_lo), core: 2. Of those that a mesh axis runs over, the one named last changes fastest.
Arguments:
- right_side: float32 [128, 128, 256], P(None, 'pa', 'pb'), may hold values from -6 to 6
- coef_x: float32 [128, 128, 256], P(None, 'pa', 'pb'), may hold values from 0.1 to 4
- coef_y: float32 [128, 128, 256], P(None, 'pa', 'pb'), may hold values from 0.1 to 4
- coef_z: float32 [128, 128, 256], P(None, 'pa', 'pb'), may hold values from 0.1 to 4
Outputs:
- solution_field: float32 [128, 128, 256], P(None, 'pa', 'pb')
- residual: float32 [128, 128, 256], P(None, 'pa', 'pb')
All inputs are finite; a program needn't handle non-finite values.
Results may differ from a plain program's by a relative error of at most 0.0003.
Values sent between devices are 32-bit elements.
A program may use at most 64 MiB of HBM per device.

v0:
```python
import math

import jax
import jax.numpy as jnp
from jax import lax
from jax.sharding import Mesh
from jax.sharding import PartitionSpec as P

ITERS = 4
PA = ("pa_0", "pa_1")
PB = ("pb_0", "pb_1", "pb_2")
PA_PB = ("pa_0", "pa_1", "pb_0", "pb_1", "pb_2")


mass_shift = 0.5
base_coef = 1.0


def padded_2(x, sides, width, wrap):
    edges = {}
    for axis, dim in sides:
        peers, length = lax.axis_size(axis), x.shape[dim]
        up = [(i, (i + 1) % peers) for i in range(peers if wrap else peers - 1)]
        last = lax.slice_in_dim(x, length - width, length, axis=dim)
        first = lax.slice_in_dim(x, 0, width, axis=dim)
        edges[dim] = lax.ppermute(last, axis, up), lax.ppermute(
            first, axis, [(b, a) for a, b in up]
        )
    done = []
    for _, dim in sides:
        low, high = edges[dim]
        around = [(width, width) if d in done else (0, 0) for d in range(x.ndim)]
        x = jnp.concatenate([jnp.pad(low, around), x, jnp.pad(high, around)], axis=dim)
        done.append(dim)
    return x


def by_axis(x, axes):
    for axis in axes:
        x = lax.psum(x, axis)
    return x


def shifted(value, axis, steps):
    count = lax.axis_size(axis)
    pairs = [(source, (source + steps) % count) for source in range(count)]
    return lax.ppermute(value, axis, pairs)


def dft_tables(points):
    positions = lax.iota(jnp.int32, points)
    product = positions[:, None] * positions[None, :] % points
    angles = product.astype(jnp.float32) * (2.0 * math.pi / points)
    return (jnp.cos(angles), jnp.sin(angles))


def apply_along(matrix, values, target_dim):
    moved = jnp.tensordot(matrix, values, axes=([1], [target_dim]), precision=lax.Precision.HIGHEST)
    return jnp.moveaxis(moved, 0, target_dim)


def forward_complex(real_part, imag_part, target_dim):
    cosine_table, sine_table = dft_tables(real_part.shape[target_dim])
    new_real = apply_along(cosine_table, real_part, target_dim) + apply_along(
        sine_table, imag_part, target_dim
    )
    new_imag = apply_along(cosine_table, imag_part, target_dim) - apply_along(
        sine_table, real_part, target_dim
    )
    return (new_real, new_imag)


def inverse_complex(real_part, imag_part, target_dim):
    points = real_part.shape[target_dim]
    cosine_table, sine_table = dft_tables(points)
    inverse_scale = 1.0 / points
    new_real = (
        apply_along(cosine_table, real_part, target_dim)
        - apply_along(sine_table, imag_part, target_dim)
    ) * inverse_scale
    new_imag = (
        apply_along(cosine_table, imag_part, target_dim)
        + apply_along(sine_table, real_part, target_dim)
    ) * inverse_scale
    return (new_real, new_imag)


def wave_term(positions, points):
    return 2.0 - 2.0 * jnp.cos(2.0 * math.pi * positions.astype(jnp.float32) / points)


def divide_symbol(real_part, imag_part, starts, totals):
    wave_x = wave_term(starts[0] + lax.iota(jnp.int32, real_part.shape[0]), totals[0])
    wave_y = wave_term(starts[1] + lax.iota(jnp.int32, real_part.shape[1]), totals[1])
    wave_z = wave_term(starts[2] + lax.iota(jnp.int32, real_part.shape[2]), totals[2])
    symbol = mass_shift + base_coef * (
        wave_x[:, None, None] + wave_y[None, :, None] + wave_z[None, None, :]
    )
    return (real_part / symbol, imag_part / symbol)


def precondition(residual):
    count_x, rows_y, rows_z = residual.shape
    groups_a = lax.axis_size(PA)
    groups_b = lax.axis_size(PB)
    total_y = rows_y * groups_a
    total_z = rows_z * groups_b
    cosine_table, sine_table = dft_tables(count_x)
    real_part = apply_along(cosine_table, residual, 0)
    imag_part = -apply_along(sine_table, residual, 0)
    devices = groups_a * groups_b
    planes = count_x // devices

    def to_slab(values):
        arranged = values.reshape(groups_a, groups_b, planes, rows_y, rows_z)
        return arranged.transpose(2, 0, 3, 1, 4).reshape(planes, total_y, total_z)

    def from_slab(values):
        arranged = values.reshape(planes, groups_a, rows_y, groups_b, rows_z)
        return arranged.transpose(1, 3, 0, 2, 4).reshape(devices, planes, rows_y, rows_z)

    stacked_real = real_part.reshape(devices, planes, rows_y, rows_z)
    stacked_imag = imag_part.reshape(devices, planes, rows_y, rows_z)
    stacked_real, stacked_imag = (
        lax.all_to_all(stacked_real, PA_PB, split_axis=0, concat_axis=0, tiled=True),
        lax.all_to_all(stacked_imag, PA_PB, split_axis=0, concat_axis=0, tiled=True),
    )
    real_part = to_slab(stacked_real)
    imag_part = to_slab(stacked_imag)
    real_part, imag_part = forward_complex(real_part, imag_part, 1)
    real_part, imag_part = forward_complex(real_part, imag_part, 2)
    starts = (lax.axis_index(PA_PB) * planes, 0, 0)
    real_part, imag_part = divide_symbol(real_part, imag_part, starts, (count_x, total_y, total_z))
    real_part, imag_part = inverse_complex(real_part, imag_part, 2)
    real_part, imag_part = inverse_complex(real_part, imag_part, 1)
    stacked_real, stacked_imag = (
        lax.all_to_all(from_slab(real_part), PA_PB, split_axis=0, concat_axis=0, tiled=True),
        lax.all_to_all(from_slab(imag_part), PA_PB, split_axis=0, concat_axis=0, tiled=True),
    )
    real_part = stacked_real.reshape(count_x, rows_y, rows_z)
    imag_part = stacked_imag.reshape(count_x, rows_y, rows_z)
    result = apply_along(cosine_table, real_part, 0) - apply_along(sine_table, imag_part, 0)
    return result * (1.0 / count_x)


def operate(grid_field, coefs, lower_coefs):
    padded = padded_2(grid_field, ((PA, 1), (PB, 2)), 1, True)
    result = mass_shift * grid_field
    result = (
        result
        + coefs[0] * (grid_field - jnp.roll(grid_field, -1, 0))
        + lower_coefs[0] * (grid_field - jnp.roll(grid_field, 1, 0))
    )
    result = (
        result
        + coefs[1] * (grid_field - padded[:, 2:, 1:-1])
        + lower_coefs[1] * (grid_field - padded[:, :-2, 1:-1])
    )
    result = (
        result
        + coefs[2] * (grid_field - padded[:, 1:-1, 2:])
        + lower_coefs[2] * (grid_field - padded[:, 1:-1, :-2])
    )
    return result


def fit_sum(residual, precond):
    return by_axis(jnp.sum(residual * precond), PA_PB)


def body(right_side, coef_x, coef_y, coef_z):
    edge_y = shifted(coef_y[:, -1:, :], PA, 1)
    edge_z = shifted(coef_z[:, :, -1:], PB, 1)
    lower_x = jnp.roll(coef_x, 1, 0)
    lower_y = jnp.concatenate([edge_y, coef_y[:, :-1, :]], axis=1)
    lower_z = jnp.concatenate([edge_z, coef_z[:, :, :-1]], axis=2)
    coefs = (coef_x, coef_y, coef_z)
    lower_coefs = (lower_x, lower_y, lower_z)
    solution_field = jnp.zeros_like(right_side)
    residual = right_side
    precond = precondition(residual)
    direction = precond
    fit_now = fit_sum(residual, precond)
    for iteration in range(ITERS):
        image_field = operate(direction, coefs, lower_coefs)
        step_size = fit_now / by_axis(jnp.sum(direction * image_field), PA_PB)
        solution_field = solution_field + step_size * direction
        residual = residual - step_size * image_field
        if iteration + 1 < ITERS:
            precond = precondition(residual)
            fit_next = fit_sum(residual, precond)
            direction = precond + fit_next / fit_now * direction
            fit_now = fit_next
    return (solution_field, residual)


def solution(mesh):
    torus = Mesh(mesh.devices.reshape(2, 4, 2, 4, 2), ("pa_0", "pa_1", "pb_0", "pb_1", "pb_2"))
    in_specs = (P(None, PA, PB), P(None, PA, PB), P(None, PA, PB), P(None, PA, PB))
    out_specs = (P(None, PA, PB), P(None, PA, PB))
    return jax.shard_map(body, mesh=torus, in_specs=in_specs, out_specs=out_specs, check_vma=False)
```

profile of v0, /device:TPU:1, one launch (start us, length us, event | category | flops | bytes accessed | tf_op | source)
XLA Modules:
  0.0 645.8 jit_solution(13919699423586263251)
XLA Ops:
  9.6 9.5 %all-to-all-start = ((f32[128,1,256]{2,1,0:T(1,128)}), f32[128,1,256]{2,1,0:T(1,128)S(1)}, u32[]{:S(2)}, u32[]{:S(2)}) async-start(f32[128,1,256]{2,1,0:T(1,128)} %reshape.614), calls=%async_computation | async-start | bytes 262144 | tf_op jit(solution)/shard_map/all_to_all | solution.py:125
  23.0 6.1 all-to-all-done
  29.2 4.7 all-to-all-start.1
  37.0 6.9 %all-to-all-done.1 = f32[128,1,256]{2,1,0:T(1,128)S(1)} async-done(((f32[128,1,256]{2,1,0:T(1,128)}), f32[128,1,256]{2,1,0:T(1,128)S(1)}, u32[]{:S(2)}, u32[]{:S(2)}) %all-to-all-start.1) | async-done | bytes 131104 | tf_op jit(solution)/shard_map/all_to_all | solution.py:126
  69.8 7.8 %all-to-all-done.2 = f32[128,1,256]{2,1,0:T(1,128)S(1)} async-done(((f32[128,1,256]{2,1,0:T(1,128)}), f32[128,1,256]{2,1,0:T(1,128)S(1)}, u32[]{:S(2)}, u32[]{:S(2)}) %all-to-all-start.2) | async-done | bytes 131104 | tf_op jit(solution)/shard_map/all_to_all | solution.py:137
  77.5 4.4 all-to-all-start.3
  84.1 7.8 %all-to-all-done.3 = f32[128,1,256]{2,1,0:T(1,128)S(1)} async-done(((f32[128,1,256]{2,1,0:T(1,128)}), f32[128,1,256]{2,1,0:T(1,128)S(1)}, u32[]{:S(2)}, u32[]{:S(2)}) %all-to-all-start.3) | async-done | bytes 131104 | tf_op jit(solution)/shard_map/all_to_all | solution.py:138
  101.6 4.4 all-reduce.12
  106.0 9.7 %all-reduce.9 = (f32[]{:T(128)}, f32[]{:T(128)}) all-reduce(f32[]{:T(128)} %get-tuple-element.12, f32[]{:T(128)} %get-tuple-element.13), channel_id=1, replica_groups=mesh['pa_0'=2,'pa_1'=4,'pb_0'=2,'pb_1'=4,'pb_2'=2] {'pa_1'}, use_global_device_ids=true, to_apply=%region_2.3 | all-reduce | flops 2 | bytes 16 | tf_op jit(solution)/shard_map/psum | solution.py:40
  115.7 5.9 all-reduce.11
  121.6 11.2 %all-reduce.8 = (f32[]{:T(128)}, f32[]{:T(128)}) all-reduce(f32[]{:T(128)} %get-tuple-element.10, f32[]{:T(128)} %get-tuple-element.11), channel_id=1, replica_groups=mesh['pa_0'=2,'pa_1'=4,'pb_0'=2,'pb_1'=4,'pb_2'=2] {'pb_1'}, use_global_device_ids=true, to_apply=%region_4.5 | all-reduce | flops 2 | bytes 16 | tf_op jit(solution)/shard_map/psum | solution.py:40
  132.8 6.4 all-reduce.10
  143.2 5.4 all-to-all-start.4
  150.1 8.4 %all-to-all-done.4 = f32[128,1,256]{2,1,0:T(1,128)S(1)} async-done(((f32[128,1,256]{2,1,0:T(1,128)}), f32[128,1,256]{2,1,0:T(1,128)S(1)}, u32[]{:S(2)}, u32[]{:S(2)}) %all-to-all-start.4) | async-done | bytes 131104 | tf_op jit(solution)/shard_map/all_to_all | solution.py:125
  158.6 4.7 all-to-all-start.5
  165.8 7.5 %all-to-all-done.5 = f32[128,1,256]{2,1,0:T(1,128)S(1)} async-done(((f32[128,1,256]{2,1,0:T(1,128)}), f32[128,1,256]{2,1,0:T(1,128)S(1)}, u32[]{:S(2)}, u32[]{:S(2)}) %all-to-all-start.5) | async-done | bytes 131104 | tf_op jit(solution)/shard_map/all_to_all | solution.py:126
  199.2 7.8 %all-to-all-done.6 = f32[128,1,256]{2,1,0:T(1,128)S(1)} async-done(((f32[128,1,256]{2,1,0:T(1,128)}), f32[128,1,256]{2,1,0:T(1,128)S(1)}, u32[]{:S(2)}, u32[]{:S(2)}) %all-to-all-start.6) | async-done | bytes 131104 | tf_op jit(solution)/shard_map/all_to_all | solution.py:137
  207.0 4.4 all-to-all-start.7
  213.6 7.8 %all-to-all-done.7 = f32[128,1,256]{2,1,0:T(1,128)S(1)} async-done(((f32[128,1,256]{2,1,0:T(1,128)}), f32[128,1,256]{2,1,0:T(1,128)S(1)}, u32[]{:S(2)}, u32[]{:S(2)}) %all-to-all-start.7) | async-done | bytes 131104 | tf_op jit(solution)/shard_map/all_to_all | solution.py:138
  224.2 4.4 psum.290
  228.6 7.3 %psum.291 = f32[]{:T(128)} all-reduce(f32[]{:T(128)} %psum.290), channel_id=1, replica_groups=mesh['pa_0'=2,'pa_1'=4,'pb_0'=2,'pb_1'=4,'pb_2'=2] {'pa_1'}, use_global_device_ids=true, to_apply=%region_14.15 | all-reduce | flops 1 | bytes 8 | tf_op jit(solution)/shard_map/psum | solution.py:40
  235.9 5.9 psum.292
  241.8 8.1 %psum.293 = f32[]{:T(128)} all-reduce(f32[]{:T(128)} %psum.292), channel_id=1, replica_groups=mesh['pa_0'=2,'pa_1'=4,'pb_0'=2,'pb_1'=4,'pb_2'=2] {'pb_1'}, use_global_device_ids=true, to_apply=%region_16.17 | all-reduce | flops 1 | bytes 8 | tf_op jit(solution)/shard_map/psum | solution.py:40
  249.9 9.5 %psum.294 = f32[]{:T(128)} all-reduce(f32[]{:T(128)} %psum.293), channel_id=1, replica_groups=mesh['pa_0'=2,'pa_1'=4,'pb_0'=2,'pb_1'=4,'pb_2'=2] {'pb_2'}, use_global_device_ids=true, to_apply=%region_17.18 | all-reduce | flops 1 | bytes 8 | tf_op jit(solution)/shard_map/psum | solution.py:40
  268.2 4.4 psum.295
  272.6 9.8 %psum.296 = f32[]{:T(128)} all-reduce(f32[]{:T(128)} %psum.295), channel_id=1, replica_groups=mesh['pa_0'=2,'pa_1'=4,'pb_0'=2,'pb_1'=4,'pb_2'=2] {'pa_1'}, use_global_device_ids=true, to_apply=%region_20.21 | all-reduce | flops 1 | bytes 8 | tf_op jit(solution)/shard_map/psum | solution.py:40
  282.4 5.9 psum.297
  288.3 10.0 %psum.298 = f32[]{:T(128)} all-reduce(f32[]{:T(128)} %psum.297), channel_id=1, replica_groups=mesh['pa_0'=2,'pa_1'=4,'pb_0'=2,'pb_1'=4,'pb_2'=2] {'pb_1'}, use_global_device_ids=true, to_apply=%region_22.23 | all-reduce | flops 1 | bytes 8 | tf_op jit(solution)/shard_map/psum | solution.py:40
  298.4 6.9 %psum.299 = f32[]{:T(128)} all-reduce(f32[]{:T(128)} %psum.298), channel_id=1, replica_groups=mesh['pa_0'=2,'pa_1'=4,'pb_0'=2,'pb_1'=4,'pb_2'=2] {'pb_2'}, use_global_device_ids=true, to_apply=%region_23.24 | all-reduce | flops 1 | bytes 8 | tf_op jit(solution)/shard_map/psum | solution.py:40
  309.2 4.9 all-to-all-start.8
  315.7 8.4 %all-to-all-done.8 = f32[128,1,256]{2,1,0:T(1,128)S(1)} async-done(((f32[128,1,256]{2,1,0:T(1,128)}), f32[128,1,256]{2,1,0:T(1,128)S(1)}, u32[]{:S(2)}, u32[]{:S(2)}) %all-to-all-start.8) | async-done | bytes 131104 | tf_op jit(solution)/shard_map/all_to_all | solution.py:125
  324.1 5.6 all-to-all-start.9
  332.9 6.7 %all-to-all-done.9 = f32[128,1,256]{2,1,0:T(1,128)} async-done(((f32[128,1,256]{2,1,0:T(1,128)}), f32[128,1,256]{2,1,0:T(1,128)}, u32[]{:S(2)}, u32[]{:S(2)}) %all-to-all-start.9) | async-done | bytes 131104 | tf_op jit(solution)/shard_map/all_to_all | solution.py:126
  367.5 7.9 %all-to-all-done.10 = f32[128,1,256]{2,1,0:T(1,128)S(1)} async-done(((f32[128,1,256]{2,1,0:T(1,128)}), f32[128,1,256]{2,1,0:T(1,128)S(1)}, u32[]{:S(2)}, u32[]{:S(2)}) %all-to-all-start.10) | async-done | bytes 131104 | tf_op jit(solution)/shard_map/all_to_all | solution.py:137
  375.3 4.4 all-to-all-start.11
  381.9 7.8 %all-to-all-done.11 = f32[128,1,256]{2,1,0:T(1,128)S(1)} async-done(((f32[128,1,256]{2,1,0:T(1,128)}), f32[128,1,256]{2,1,0:T(1,128)S(1)}, u32[]{:S(2)}, u32[]{:S(2)}) %all-to-all-start.11) | async-done | bytes 131104 | tf_op jit(solution)/shard_map/all_to_all | solution.py:138
  392.6 4.4 psum.300
  397.0 7.3 %psum.301 = f32[]{:T(128)} all-reduce(f32[]{:T(128)} %psum.300), channel_id=1, replica_groups=mesh['pa_0'=2,'pa_1'=4,'pb_0'=2,'pb_1'=4,'pb_2'=2] {'pa_1'}, use_global_device_ids=true, to_apply=%region_26.27 | all-reduce | flops 1 | bytes 8 | tf_op jit(solution)/shard_map/psum | solution.py:40
  404.3 5.9 psum.302
  410.2 8.1 %psum.303 = f32[]{:T(128)} all-reduce(f32[]{:T(128)} %psum.302), channel_id=1, replica_groups=mesh['pa_0'=2,'pa_1'=4,'pb_0'=2,'pb_1'=4,'pb_2'=2] {'pb_1'}, use_global_device_ids=true, to_apply=%region_28.29 | all-reduce | flops 1 | bytes 8 | tf_op jit(solution)/shard_map/psum | solution.py:40
  418.3 9.5 %psum.304 = f32[]{:T(128)} all-reduce(f32[]{:T(128)} %psum.303), channel_id=1, replica_groups=mesh['pa_0'=2,'pa_1'=4,'pb_0'=2,'pb_1'=4,'pb_2'=2] {'pb_2'}, use_global_device_ids=true, to_apply=%region_29.30 | all-reduce | flops 1 | bytes 8 | tf_op jit(solution)/shard_map/psum | solution.py:40
  436.4 4.4 psum.305
  440.8 9.9 %psum.306 = f32[]{:T(128)} all-reduce(f32[]{:T(128)} %psum.305), channel_id=1, replica_groups=mesh['pa_0'=2,'pa_1'=4,'pb_0'=2,'pb_1'=4,'pb_2'=2] {'pa_1'}, use_global_device_ids=true, to_apply=%region_32.33 | all-reduce | flops 1 | bytes 8 | tf_op jit(solution)/shard_map/psum | solution.py:40
  450.6 5.9 psum.307
  456.5 10.0 %psum.308 = f32[]{:T(128)} all-reduce(f32[]{:T(128)} %psum.307), channel_id=1, replica_groups=mesh['pa_0'=2,'pa_1'=4,'pb_0'=2,'pb_1'=4,'pb_2'=2] {'pb_1'}, use_global_device_ids=true, to_apply=%region_34.35 | all-reduce | flops 1 | bytes 8 | tf_op jit(solution)/shard_map/psum | solution.py:40
  466.6 6.9 %psum.309 = f32[]{:T(128)} all-reduce(f32[]{:T(128)} %psum.308), channel_id=1, replica_groups=mesh['pa_0'=2,'pa_1'=4,'pb_0'=2,'pb_1'=4,'pb_2'=2] {'pb_2'}, use_global_device_ids=true, to_apply=%region_35.36 | all-reduce | flops 1 | bytes 8 | tf_op jit(solution)/shard_map/psum | solution.py:40
  477.3 4.9 all-to-all-start.12
  483.8 8.4 %all-to-all-done.12 = f32[128,1,256]{2,1,0:T(1,128)S(1)} async-done(((f32[128,1,256]{2,1,0:T(1,128)}), f32[128,1,256]{2,1,0:T(1,128)S(1)}, u32[]{:S(2)}, u32[]{:S(2)}) %all-to-all-start.12) | async-done | bytes 131104 | tf_op jit(solution)/shard_map/all_to_all | solution.py:125
  492.2 5.6 all-to-all-start.13
  501.0 6.7 %all-to-all-done.13 = f32[128,1,256]{2,1,0:T(1,128)} async-done(((f32[128,1,256]{2,1,0:T(1,128)}), f32[128,1,256]{2,1,0:T(1,128)}, u32[]{:S(2)}, u32[]{:S(2)}) %all-to-all-start.13) | async-done | bytes 131104 | tf_op jit(solution)/shard_map/all_to_all | solution.py:126
  529.2 5.3 all-to-all-start.14
  536.8 7.6 %all-to-all-done.14 = f32[128,1,256]{2,1,0:T(1,128)} async-done(((f32[128,1,256]{2,1,0:T(1,128)}), f32[128,1,256]{2,1,0:T(1,128)}, u32[]{:S(2)}, u32[]{:S(2)}) %all-to-all-start.14) | async-done | bytes 131104 | tf_op jit(solution)/shard_map/all_to_all | solution.py:137
  544.4 4.4 all-to-all-start.15
  552.0 6.9 %all-to-all-done.15 = f32[128,1,256]{2,1,0:T(1,128)S(1)} async-done(((f32[128,1,256]{2,1,0:T(1,128)}), f32[128,1,256]{2,1,0:T(1,128)S(1)}, u32[]{:S(2)}, u32[]{:S(2)}) %all-to-all-start.15) | async-done | bytes 131104 | tf_op jit(solution)/shard_map/all_to_all | solution.py:138
  561.7 4.4 psum.310
  566.1 7.3 %psum.311 = f32[]{:T(128)} all-reduce(f32[]{:T(128)} %psum.310), channel_id=1, replica_groups=mesh['pa_0'=2,'pa_1'=4,'pb_0'=2,'pb_1'=4,'pb_2'=2] {'pa_1'}, use_global_device_ids=true, to_apply=%region_38.39 | all-reduce | flops 1 | bytes 8 | tf_op jit(solution)/shard_map/psum | solution.py:40
  573.4 5.9 psum.312
  579.3 8.1 %psum.313 = f32[]{:T(128)} all-reduce(f32[]{:T(128)} %psum.312), channel_id=1, replica_groups=mesh['pa_0'=2,'pa_1'=4,'pb_0'=2,'pb_1'=4,'pb_2'=2] {'pb_1'}, use_global_device_ids=true, to_apply=%region_40.41 | all-reduce | flops 1 | bytes 8 | tf_op jit(solution)/shard_map/psum | solution.py:40
  587.4 9.5 %psum.314 = f32[]{:T(128)} all-reduce(f32[]{:T(128)} %psum.313), channel_id=1, replica_groups=mesh['pa_0'=2,'pa_1'=4,'pb_0'=2,'pb_1'=4,'pb_2'=2] {'pb_2'}, use_global_device_ids=true, to_apply=%region_41.42 | all-reduce | flops 1 | bytes 8 | tf_op jit(solution)/shard_map/psum | solution.py:40
  605.9 4.7 psum.315
  610.5 7.2 %psum.316 = f32[]{:T(128)} all-reduce(f32[]{:T(128)} %psum.315), channel_id=1, replica_groups=mesh['pa_0'=2,'pa_1'=4,'pb_0'=2,'pb_1'=4,'pb_2'=2] {'pa_1'}, use_global_device_ids=true, to_apply=%region_44.45 | all-reduce | flops 1 | bytes 8 | tf_op jit(solution)/shard_map/psum | solution.py:40
  617.7 5.9 psum.317
  623.6 9.5 %psum.318 = f32[]{:T(128)} all-reduce(f32[]{:T(128)} %psum.317), channel_id=1, replica_groups=mesh['pa_0'=2,'pa_1'=4,'pb_0'=2,'pb_1'=4,'pb_2'=2] {'pb_1'}, use_global_device_ids=true, to_apply=%region_46.47 | all-reduce | flops 1 | bytes 8 | tf_op jit(solution)/shard_map/psum | solution.py:40
  633.1 10.3 %psum.319 = f32[]{:T(128)} all-reduce(f32[]{:T(128)} %psum.318), channel_id=1, replica_groups=mesh['pa_0'=2,'pa_1'=4,'pb_0'=2,'pb_1'=4,'pb_2'=2] {'pb_2'}, use_global_device_ids=true, to_apply=%region_47.48 | all-reduce | flops 1 | bytes 8 | tf_op jit(solution)/shard_map/psum | solution.py:40
  (297 shorter events, 190.6 us)
Async XLA Ops:
  2.1 94.3 %collective-permute-start.4 = (f32[128,16,1]{0,2,1:T(1,128)}, f32[128,16,1]{0,2,1:T(1,128)S(1)}, u32[]{:S(2)}, u32[]{:S(2)}) collective-permute-start(f32[128,16,1]{0,2,1:T(1,128)} %slice.196), channel_id=1, source_target_pairs={{0,1},{1,2},{2,3},{3,4},{4,5},{5,6},{6,7},{7,8},{8,9},{9,10},{10,1... | collective-permute-start | bytes 24584 | tf_op jit(solution)/shard_map/ppermute | solution.py:47
  5.4 94.4 %collective-permute-start.1 = (f32[128,1,16]{0,2,1:T(8,128)S(1)}, f32[128,1,16]{0,2,1:T(8,128)S(1)}, u32[]{:S(2)}, u32[]{:S(2)}) collective-permute-start(f32[128,1,16]{0,2,1:T(8,128)S(1)} %slice.190), channel_id=1, source_target_pairs={{0,16},{16,32},{32,48},{48,64},{64,80},{80,96},{96,112},{112,0},{1... | collective-permute-start | bytes 24584 | tf_op jit(solution)/shard_map/ppermute | solution.py:47
  9.6 9.5 %copy-start.7 = (f32[128,16,16]{0,2,1:T(8,128)S(1)}, f32[128,16,16]{0,2,1:T(8,128)}, u32[]{:S(2)}) copy-start(f32[128,16,16]{0,2,1:T(8,128)} %param.4) | copy-start | bytes 393220
  9.6 19.5 %all-to-all-start = ((f32[128,1,256]{2,1,0:T(1,128)}), f32[128,1,256]{2,1,0:T(1,128)S(1)}, u32[]{:S(2)}, u32[]{:S(2)}) async-start(f32[128,1,256]{2,1,0:T(1,128)} %reshape.614), calls=%async_computation | async-start | bytes 262144 | tf_op jit(solution)/shard_map/all_to_all | solution.py:125
  19.8 0.9 copy-start.2
  19.8 0.9 copy-start.1
  29.2 14.7 %all-to-all-start.1 = ((f32[128,1,256]{2,1,0:T(1,128)}), f32[128,1,256]{2,1,0:T(1,128)S(1)}, u32[]{:S(2)}, u32[]{:S(2)}) async-start(f32[128,1,256]{2,1,0:T(1,128)} %reshape.616), calls=%async_computation.1 | async-start | bytes 262144 | tf_op jit(solution)/shard_map/all_to_all | solution.py:126
  49.0 1.6 copy-start.16
  49.0 1.6 copy-start.18
  63.2 14.3 %all-to-all-start.2 = ((f32[128,1,256]{2,1,0:T(1,128)}), f32[128,1,256]{2,1,0:T(1,128)S(1)}, u32[]{:S(2)}, u32[]{:S(2)}) async-start(f32[128,1,256]{2,1,0:T(1,128)} %reshape.618), calls=%async_computation.2 | async-start | bytes 262144 | tf_op jit(solution)/shard_map/all_to_all | solution.py:137
  77.5 14.4 %all-to-all-start.3 = ((f32[128,1,256]{2,1,0:T(1,128)}), f32[128,1,256]{2,1,0:T(1,128)S(1)}, u32[]{:S(2)}, u32[]{:S(2)}) async-start(f32[128,1,256]{2,1,0:T(1,128)} %reshape.620), calls=%async_computation.3 | async-start | bytes 262144 | tf_op jit(solution)/shard_map/all_to_all | solution.py:138
  94.3 5.5 collective-permute-start.3
  95.2 4.7 collective-permute-start.5
  96.1 4.6 collective-permute-start.2
  96.4 4.3 copy-start
  96.4 4.3 collective-permute-start
  143.2 15.4 %all-to-all-start.4 = ((f32[128,1,256]{2,1,0:T(1,128)}), f32[128,1,256]{2,1,0:T(1,128)S(1)}, u32[]{:S(2)}, u32[]{:S(2)}) async-start(f32[128,1,256]{2,1,0:T(1,128)} %reshape.622), calls=%async_computation.4 | async-start | bytes 262144 | tf_op jit(solution)/shard_map/all_to_all | solution.py:125
  158.6 14.7 %all-to-all-start.5 = ((f32[128,1,256]{2,1,0:T(1,128)}), f32[128,1,256]{2,1,0:T(1,128)S(1)}, u32[]{:S(2)}, u32[]{:S(2)}) async-start(f32[128,1,256]{2,1,0:T(1,128)} %reshape.624), calls=%async_computation.5 | async-start | bytes 262144 | tf_op jit(solution)/shard_map/all_to_all | solution.py:126
  178.4 1.6 copy-start.17
  178.4 1.6 copy-start.19
  192.6 14.3 %all-to-all-start.6 = ((f32[128,1,256]{2,1,0:T(1,128)}), f32[128,1,256]{2,1,0:T(1,128)S(1)}, u32[]{:S(2)}, u32[]{:S(2)}) async-start(f32[128,1,256]{2,1,0:T(1,128)} %reshape.626), calls=%async_computation.6 | async-start | bytes 262144 | tf_op jit(solution)/shard_map/all_to_all | solution.py:137
  207.0 14.4 %all-to-all-start.7 = ((f32[128,1,256]{2,1,0:T(1,128)}), f32[128,1,256]{2,1,0:T(1,128)S(1)}, u32[]{:S(2)}, u32[]{:S(2)}) async-start(f32[128,1,256]{2,1,0:T(1,128)} %reshape.628), calls=%async_computation.7 | async-start | bytes 262144 | tf_op jit(solution)/shard_map/all_to_all | solution.py:138
  261.0 5.5 collective-permute-start.8
  261.4 5.1 collective-permute-start.9
  262.8 4.6 collective-permute-start.7
  263.5 4.0 collective-permute-start.6
  306.6 85.3 %copy-start.3 = (f32[128,16,16]{0,2,1:T(8,128)}, f32[128,16,16]{0,2,1:T(8,128)S(1)}, u32[]{:S(2)}) copy-start(f32[128,16,16]{0,2,1:T(8,128)S(1)} %multiply_subtract_fusion.2) | copy-start | bytes 393220
  309.2 14.9 %all-to-all-start.8 = ((f32[128,1,256]{2,1,0:T(1,128)}), f32[128,1,256]{2,1,0:T(1,128)S(1)}, u32[]{:S(2)}, u32[]{:S(2)}) async-start(f32[128,1,256]{2,1,0:T(1,128)} %reshape.630), calls=%async_computation.8 | async-start | bytes 262144 | tf_op jit(solution)/shard_map/all_to_all | solution.py:125
  324.1 15.5 %all-to-all-start.9 = ((f32[128,1,256]{2,1,0:T(1,128)}), f32[128,1,256]{2,1,0:T(1,128)}, u32[]{:S(2)}, u32[]{:S(2)}) async-start(f32[128,1,256]{2,1,0:T(1,128)} %reshape.632), calls=%async_computation.9 | async-start | bytes 262144 | tf_op jit(solution)/shard_map/all_to_all | solution.py:126
  342.6 0.9 copy-start.14
  355.0 3.1 copy-start.8
  360.9 4.3 copy-start.9
  360.9 4.3 copy-start.12
  360.9 14.4 %all-to-all-start.10 = ((f32[128,1,256]{2,1,0:T(1,128)}), f32[128,1,256]{2,1,0:T(1,128)S(1)}, u32[]{:S(2)}, u32[]{:S(2)}) async-start(f32[128,1,256]{2,1,0:T(1,128)} %reshape.634), calls=%async_computation.10 | async-start | bytes 262144 | tf_op jit(solution)/shard_map/all_to_all | solution.py:137
  375.3 14.4 %all-to-all-start.11 = ((f32[128,1,256]{2,1,0:T(1,128)}), f32[128,1,256]{2,1,0:T(1,128)S(1)}, u32[]{:S(2)}, u32[]{:S(2)}) async-start(f32[128,1,256]{2,1,0:T(1,128)} %reshape.636), calls=%async_computation.11 | async-start | bytes 262144 | tf_op jit(solution)/shard_map/all_to_all | solution.py:138
  429.2 5.5 collective-permute-start.12
  429.6 5.1 collective-permute-start.13
  431.0 4.6 collective-permute-start.11
  431.6 3.9 collective-permute-start.10
  435.6 39.1 %copy-start.4 = (f32[128,16,16]{0,2,1:T(8,128)S(1)}, f32[128,16,16]{0,2,1:T(8,128)}, u32[]{:S(2)}) copy-start(f32[128,16,16]{0,2,1:T(8,128)} %copy-done.3) | copy-start | bytes 393220
  477.3 14.9 %all-to-all-start.12 = ((f32[128,1,256]{2,1,0:T(1,128)}), f32[128,1,256]{2,1,0:T(1,128)S(1)}, u32[]{:S(2)}, u32[]{:S(2)}) async-start(f32[128,1,256]{2,1,0:T(1,128)} %reshape.638), calls=%async_computation.12 | async-start | bytes 262144 | tf_op jit(solution)/shard_map/all_to_all | solution.py:125
  492.2 15.5 %all-to-all-start.13 = ((f32[128,1,256]{2,1,0:T(1,128)}), f32[128,1,256]{2,1,0:T(1,128)}, u32[]{:S(2)}, u32[]{:S(2)}) async-start(f32[128,1,256]{2,1,0:T(1,128)} %reshape.640), calls=%async_computation.13 | async-start | bytes 262144 | tf_op jit(solution)/shard_map/all_to_all | solution.py:126
  499.9 1.2 copy-start.5
  510.7 0.9 copy-start.15
  511.6 0.9 copy-start.6
  523.5 3.0 copy-start.10
  529.2 5.3 copy-start.11
  529.2 5.3 copy-start.13
  529.2 15.2 %all-to-all-start.14 = ((f32[128,1,256]{2,1,0:T(1,128)}), f32[128,1,256]{2,1,0:T(1,128)}, u32[]{:S(2)}, u32[]{:S(2)}) async-start(f32[128,1,256]{2,1,0:T(1,128)} %reshape.642), calls=%async_computation.14 | async-start | bytes 262144 | tf_op jit(solution)/shard_map/all_to_all | solution.py:137
  544.4 14.4 %all-to-all-start.15 = ((f32[128,1,256]{2,1,0:T(1,128)}), f32[128,1,256]{2,1,0:T(1,128)S(1)}, u32[]{:S(2)}, u32[]{:S(2)}) async-start(f32[128,1,256]{2,1,0:T(1,128)} %reshape.644), calls=%async_computation.15 | async-start | bytes 262144 | tf_op jit(solution)/shard_map/all_to_all | solution.py:138
  598.3 5.5 collective-permute-start.15
  599.1 4.8 collective-permute-start.14
  602.0 3.1 collective-permute-start.16
  602.9 2.2 collective-permute-start.17
where the time goes:
time: 652 us; the launch traced here: 646 us
  blocking collectives  255 us (39%)
  waiting for transfers between devices  124 us (19%)
  starting transfers between devices  107 us (16%)
  matrix products  77.7 us (12%)
  local copies, waits for them, and re-layouts  45.4 us (7%)
  other arithmetic  25 us (4%)
  between operations  11.7 us (2%)
    psum x35, blocking collectives, by_axis(): x = lax.psum(x, axis)  255 us
    dot_general x64, matrix products, apply_along(): jnp.tensordot(matrix, values, axes=([1], [target_dim]), precision=lax.Pre...  68.5 us
    all_to_all x4, waiting for transfers between devices, precondition(): lax.all_to_all(stacked_real, PA_PB, split_axis=0, concat_axis=0, tiled=True)  31.4 us
    all_to_all x4, waiting for transfers between devices, precondition(): lax.all_to_all(from_slab(real_part), PA_PB, split_axis=0, concat_axis=0,...  31.1 us
    all_to_all x4, waiting for transfers between devices, precondition(): lax.all_to_all(from_slab(imag_part), PA_PB, split_axis=0, concat_axis=0,...  30.3 us
    all_to_all x4, waiting for transfers between devices, precondition(): lax.all_to_all(stacked_imag, PA_PB, split_axis=0, concat_axis=0, tiled=True)  27.7 us
    all_to_all x4, starting transfers between devices, precondition(): lax.all_to_all(stacked_real, PA_PB, split_axis=0, concat_axis=0, tiled=True)  24.8 us
    unnamed x72, local copies, waits for them, and re-layouts  23.5 us
  transfers between devices with their start and end apart: 34, of which 20 were waited for; matrix products, arithmetic and copies ran while one was open for 10% of the time, Pallas kernels for 0%

commit v1 on v0

v1 whole, which is shorter than its diff:
```python
import functools

import jax
import jax.numpy as jnp
import numpy as np
from jax import lax
from jax.experimental import pallas as pl
from jax.experimental.pallas import tpu as pltpu
from jax.sharding import PartitionSpec as P

ITERS = 4
NA = 8
NB = 16
ND = NA * NB
MESH = pl.DeviceIdType.MESH
mass_shift = 0.5
base_coef = 1.0


def cas_matrix(points):
    index = np.arange(points)
    angle = 2.0 * np.pi * ((index[:, None] * index[None, :]) % points) / points
    return (np.cos(angle) + np.sin(angle)) / np.sqrt(points)


def split_constant(matrix):
    high = jnp.asarray(matrix, jnp.float32).astype(jnp.bfloat16)
    low = (jnp.asarray(matrix, jnp.float32) - high.astype(jnp.float32)).astype(jnp.bfloat16)
    return high, low


def wave(points):
    return 2.0 - 2.0 * np.cos(2.0 * np.pi * np.arange(points) / points)


def ring_distance(step):
    return min(step, 4 - step)


OFFSETS = [
    (dx, dy, dz, dc)
    for dx in range(4)
    for dy in range(4)
    for dz in range(4)
    for dc in range(2)
    if (dx, dy, dz, dc) != (0, 0, 0, 0)
]
OFFSETS.sort(
    key=lambda o: -(ring_distance(o[0]) + ring_distance(o[1]) + ring_distance(o[2]) + 0.5 * o[3])
)


def split(value):
    high = value.astype(jnp.bfloat16)
    low = (value - high.astype(jnp.float32)).astype(jnp.bfloat16)
    return high, low


def product(left, right, dims):
    def one(a, b):
        return lax.dot_general(a, b, (dims, ((), ())), preferred_element_type=jnp.float32)

    return one(left[0], right[0]) + (one(left[1], right[0]) + one(left[0], right[1]))


def lanes_to(value, index):
    return jnp.take_along_axis(value, index, axis=1)


def segment_transpose(value):
    rows = value.shape[0]
    row = lax.broadcasted_iota(jnp.int32, (8, 128), 0)
    lane = lax.broadcasted_iota(jnp.int32, (8, 128), 1)
    group, inner = lane // 16, lane % 16
    first = ((row + group) % 8) * 16 + inner
    middle = (row - group + 8) % 8
    last = ((row - group + 8) % 8) * 16 + inner
    done = []
    for start in range(0, rows, 8):
        tile = value[start : start + 8]
        tile = jnp.take_along_axis(tile, first, axis=1)
        tile = jnp.take_along_axis(tile, middle, axis=0)
        done.append(jnp.take_along_axis(tile, last, axis=1))
    return done


def kernel(
    b_ref, cx_ref, cy_ref, cz_ref, h1h_ref, h1l_ref, h2h_ref, h2l_ref, wy_ref, wz_ref,
    x_ref, r_ref,
    fs, fr, bs, br, lx_ref, ly_ref, lz_ref, diag_ref, zlast, ylow, zlow, inv_ref,
    rhat, shat, u_ref, w_ref, p_ref, s_ref, sc,
    f_send, f_recv, b_send, b_recv, e_sems,
):
    a = lax.axis_index("pa")
    b = lax.axis_index("pb")
    me = a * NB + b
    at_y, at_x, core = lax.rem(a, 4), lax.rem(b // 2, 4), lax.rem(b, 2)
    at_z = (b // 8) * 2 + a // 4
    part_x = [lax.rem(at_x + d, 4) * 2 for d in range(4)]
    part_y = [lax.rem(at_y + d, 4) for d in range(4)]
    part_za = [lax.rem(lax.rem(at_z + d, 4), 2) * 4 for d in range(4)]
    part_zb = [(lax.rem(at_z + d, 4) // 2) * 8 for d in range(4)]
    part_c = [core, 1 - core]

    def targets():
        for dx, dy, dz, dc in OFFSETS:
            yield part_za[dz] + part_y[dy], part_zb[dz] + part_x[dx] + part_c[dc]

    def exchange(source, target, send_sem, recv_sem):
        for ta, tb in targets():
            pltpu.make_async_remote_copy(
                source.at[ta * NB + tb], target.at[me], send_sem, recv_sem,
                device_id=(ta, tb), device_id_type=MESH,
            ).start()
        target[pl.ds(me, 1)] = source[pl.ds(me, 1)]

    def all_others(buffer, sem):
        part = buffer.at[pl.ds(0, ND - 1)]
        pltpu.make_async_copy(part, part, sem).wait()

    barrier = pltpu.get_barrier_semaphore()
    for ta, tb in targets():
        pl.semaphore_signal(barrier, inc=1, device_id=(ta, tb), device_id_type=MESH)

    h1 = (h1h_ref[...], h1l_ref[...])
    h2 = (h2h_ref[...], h2l_ref[...])

    def send_lines(field, partial):
        lines = product(h1, split(field), ((1,), (1,)))
        fs[:, 0, :] = lines[:, :128]
        fs[:, 1, :] = lines[:, 128:]
        fs[:, 2, :] = jnp.broadcast_to(partial, (ND, 128))
        exchange(fs, fr, f_send, f_recv)

    rhs = b_ref[...]
    zlast[...] = cz_ref[...].reshape(16, 16, 128)[:, 15, :]
    r_ref[...] = rhs
    zero = jnp.zeros((256, 128), jnp.float32)
    for ref in (x_ref, u_ref, w_ref, p_ref, s_ref):
        ref[...] = zero
    rhat[...] = jnp.zeros_like(rhat)
    shat[...] = jnp.zeros_like(shat)

    pl.semaphore_wait(barrier, ND - 1)
    send_lines(rhs, jnp.zeros((1, 128), jnp.float32))
    edge_y = pltpu.make_async_remote_copy(
        cy_ref.at[pl.ds(240, 16)], ylow, e_sems.at[0], e_sems.at[1],
        device_id=(lax.rem(a + 1, NA), b), device_id_type=MESH,
    )
    edge_z = pltpu.make_async_remote_copy(
        zlast, zlow, e_sems.at[2], e_sems.at[3],
        device_id=(a, lax.rem(b + 1, NB)), device_id_type=MESH,
    )
    edge_y.start()
    edge_z.start()

    symbol = mass_shift + base_coef * (
        wy_ref[pl.ds(me, 1), 0:1] + wy_ref[:, 0:1] + wz_ref[...]
    )
    inv_ref[...] = 1.0 / symbol

    def below_z(field, edge):
        cube = field.reshape(16, 16, 128)
        return jnp.concatenate([edge[:, None, :], cube[:, :15]], axis=1).reshape(256, 128)

    def above_z(field, edge):
        cube = field.reshape(16, 16, 128)
        return jnp.concatenate([cube[:, 1:], edge[:, None, :]], axis=1).reshape(256, 128)

    edge_y.wait()
    edge_z.wait()
    cx, cy, cz = cx_ref[...], cy_ref[...], cz_ref[...]
    lower_x = pltpu.roll(cx, 1, 1)
    lower_y = jnp.concatenate([ylow[...], cy[:240]], axis=0)
    lower_z = below_z(cz, zlow[...])
    lx_ref[...] = lower_x
    ly_ref[...] = lower_y
    lz_ref[...] = lower_z
    diag_ref[...] = mass_shift + ((cx + lower_x) + (cy + lower_y) + (cz + lower_z))

    lane = lax.broadcasted_iota(jnp.int32, (128, 128), 1)
    lane_row = lax.broadcasted_iota(jnp.int32, (1, 128), 1)
    low_half = jnp.where(
        lane < 32, lane % 16, jnp.where(lane < 48, (lane % 8) * 16 + 15, (lane % 8) * 16)
    )
    high_half = jnp.where(
        lane < 32, lane % 16 + 112, jnp.where(lane < 48, (lane % 8) * 16 + 15, (lane % 8) * 16)
    )
    from_high = (lane < 16) | ((lane >= 32) & (lane % 16 >= 8))

    def slab(step, beta):
        tiles = [segment_transpose(fr[:, half, :]) for half in range(2)]
        plane = jnp.concatenate(
            [
                jnp.concatenate(
                    [tiles[half][2 * row + part] for row in range(NA) for half in range(2)], axis=0
                )
                for part in range(2)
            ],
            axis=1,
        )
        freq = product(split(plane), h2, ((1,), (0,)))
        freq = product(h1, split(freq), ((1,), (0,)))
        new_s = freq + beta * shat[...]
        new_r = rhat[...] - step * new_s
        shat[...] = new_s
        rhat[...] = new_r
        scaled = new_r * inv_ref[...]
        part_fit = jnp.sum(new_r * scaled, keepdims=True)
        back = product(h1, split(scaled), ((1,), (0,)))
        back = product(split(back), h2, ((1,), (0,)))
        out = [segment_transpose(back[:, part * 128 : part * 128 + 128]) for part in range(2)]
        halves = [
            jnp.concatenate(
                [out[part][2 * row + half] for row in range(NA) for part in range(2)], axis=0
            )
            for half in range(2)
        ]
        edges = jnp.where(
            from_high, lanes_to(halves[1], high_half), lanes_to(halves[0], low_half)
        )
        cube = edges.reshape(NA, NB, 128)
        from_low_z = jnp.concatenate([cube[:, 15:], cube[:, :15]], axis=1).reshape(ND, 128)
        from_high_z = jnp.concatenate([cube[:, 1:], cube[:, :1]], axis=1).reshape(ND, 128)
        from_low_y = jnp.concatenate([edges[112:], edges[:112]], axis=0)
        from_high_y = jnp.concatenate([edges[16:], edges[:16]], axis=0)
        halo = jnp.where(
            lane < 32,
            jnp.where(lane < 16, from_low_y, from_high_y),
            jnp.where(lane < 48, from_low_z, from_high_z),
        )
        bs[:, 0, :] = halves[0]
        bs[:, 1, :] = halves[1]
        bs[:, 2, :] = jnp.where(lane < 64, halo, jnp.broadcast_to(part_fit, (ND, 128)))
        exchange(bs, br, b_send, b_recv)

    def scalars(turn, fit, fit_old, step_old, curvature):
        beta = jnp.where(turn <= 1, 0.0, fit / fit_old)
        step = fit / (curvature - jnp.where(turn <= 1, 0.0, beta * fit / step_old))
        return jnp.where(turn == 0, -1.0, step), beta

    def update(step, beta):
        new_p = u_ref[...] + beta * p_ref[...]
        new_s = w_ref[...] + beta * s_ref[...]
        p_ref[...] = new_p
        s_ref[...] = new_s
        x_ref[...] = x_ref[...] + step * new_p
        r_ref[...] = r_ref[...] - step * new_s

    def turn_body(turn, carry):
        fit, fit_old, step_old = sc[0:1], sc[1:2], sc[2:3]
        all_others(fr, f_recv)
        curvature = jnp.sum(fr[:, 2, :], axis=0, keepdims=True)
        step, beta = scalars(turn, fit, fit_old, step_old, curvature)
        slab(step[:, 0:1], beta[:, 0:1])
        update(step, beta)

        all_others(br, b_recv)
        total = jnp.sum(br[:, 2, :], axis=0, keepdims=True)
        new_fit = jnp.where(lane_row < 64, pltpu.roll(total, 64, 1), total)
        lines = [product(split(br[:, k, :]), h1, ((0,), (0,))) for k in range(3)]
        u = jnp.concatenate(lines[:2], axis=0)
        halo = lines[2]
        u_ref[...] = u
        image = diag_ref[...] * u
        image -= cx_ref[...] * pltpu.roll(u, 127, 1)
        image -= lx_ref[...] * pltpu.roll(u, 1, 1)
        image -= cy_ref[...] * jnp.concatenate([u[16:], halo[16:32]], axis=0)
        image -= ly_ref[...] * jnp.concatenate([halo[0:16], u[:240]], axis=0)
        image -= cz_ref[...] * above_z(u, halo[48:64])
        image -= lz_ref[...] * below_z(u, halo[32:48])
        w_ref[...] = image
        all_others(fs, f_send)
        send_lines(image, jnp.sum(u * image, keepdims=True))
        all_others(bs, b_send)
        sc[0:1] = new_fit
        sc[1:2] = fit
        sc[2:3] = step
        return carry

    sc[...] = jnp.ones_like(sc)
    lax.fori_loop(0, ITERS, turn_body, 0)
    fit, fit_old, step_old = sc[0:1], sc[1:2], sc[2:3]
    all_others(fr, f_recv)
    curvature = jnp.sum(fr[:, 2, :], axis=0, keepdims=True)
    step, beta = scalars(ITERS, fit, fit_old, step_old, curvature)
    update(step, beta)
    all_others(fs, f_send)


def body(right_side, coef_x, coef_y, coef_z):
    def lines(value):
        return value.transpose(1, 2, 0).reshape(256, 128)

    h1 = split_constant(cas_matrix(128))
    h2 = split_constant(cas_matrix(256))
    wave_y = jnp.asarray(np.broadcast_to(wave(128)[:, None], (128, 128)), jnp.float32)
    wave_z = jnp.asarray(wave(256)[None, :], jnp.float32)
    message = pltpu.VMEM((ND, 3, 128), jnp.float32)
    block = pltpu.VMEM((256, 128), jnp.float32)
    plane = pltpu.VMEM((128, 256), jnp.float32)
    edge = pltpu.VMEM((16, 128), jnp.float32)
    vmem = pl.BlockSpec(memory_space=pltpu.VMEM)
    x, r = pl.pallas_call(
        kernel,
        out_shape=[jax.ShapeDtypeStruct((256, 128), jnp.float32)] * 2,
        in_specs=[vmem] * 10,
        out_specs=[vmem] * 2,
        scratch_shapes=[message] * 4 + [block] * 4 + [edge] * 3 + [plane] * 3 + [block] * 4
        + [pltpu.VMEM((8, 128), jnp.float32)]
        + [pltpu.SemaphoreType.DMA] * 4 + [pltpu.SemaphoreType.DMA((4,))],
        compiler_params=pltpu.CompilerParams(collective_id=0, has_side_effects=True),
    )(
        lines(right_side), lines(coef_x), lines(coef_y), lines(coef_z),
        h1[0], h1[1], h2[0], h2[1], wave_y, wave_z,
    )

    def block_of(value):
        return value.reshape(16, 16, 128).transpose(2, 0, 1)

    return block_of(x), block_of(r)


def solution(mesh):
    spec = P(None, "pa", "pb")
    return jax.shard_map(
        body, mesh=mesh, in_specs=(spec,) * 4, out_specs=(spec,) * 2, check_vma=False
    )
```

time: 652 us -> 80.7 us (0.12)
  blocking collectives: 255 us -> 0 us
  waiting for transfers between devices: 124 us -> 0 us
  starting transfers between devices: 107 us -> 0 us
  matrix products: 77.7 us -> 0 us
  Pallas kernels: 0 us -> 77.7 us
  local copies, waits for them, and re-layouts: 45.4 us -> 2.26 us
  other arithmetic: 25 us -> 0 us
  between operations: 11.7 us -> 0.65 us
    psum x35 -> x0, blocking collectives: 255 us -> none  [by_axis(): x = lax.psum(x, axis)]
    all_to_all x16 -> x0, waiting for transfers between devices: 120 us -> none  [the longest x4 31.4 us: precondition(): lax.all_to_all(stacked_real, PA_PB, split_axis=0, concat_axis=0, tiled=True)]
    all_to_all x16 -> x0, starting transfers between devices: 81.3 us -> none  [the longest x4 24.8 us: precondition(): lax.all_to_all(stacked_real, PA_PB, split_axis=0, concat_axis=0, tiled=True)]
    pallas_call x0 -> x1, Pallas kernels: none -> 77.7 us  [body(): pl.pallas_call(kernel, out_shape=[jax.ShapeDtypeStruct((256, 128), jnp.fl...]
    dot_general x64 -> x0, matrix products: 68.5 us -> none  [apply_along(): jnp.tensordot(matrix, values, axes=([1], [target_dim]), precision=lax.Pre...]
    ppermute x18 -> x0, starting transfers between devices: 25.5 us -> none  [the longest x8 14.6 us: padded_2(): lax.ppermute(first, axis, [(b, a) for a, b in up])]
    unnamed x72 -> x4, local copies, waits for them, and re-layouts: 23.5 us -> 2.26 us
    all_to_all x16 -> x0, other arithmetic: 17.6 us -> none  [the longest x4 5.52 us: precondition(): lax.all_to_all(stacked_imag, PA_PB, split_axis=0, concat_axis=0, tiled=True)]
  transfers between devices with their start and end apart: 34 -> 0, of which waited for: 20 -> 0; matrix products, arithmetic and copies ran while one was open for 10% -> 0% of each run, Pallas kernels for 0% -> 0%
where the time goes in v1:
time: 80.7 us; the launch traced here: 80.6 us
  Pallas kernels  77.7 us (96%)
  local copies, waits for them, and re-layouts  2.26 us (3%)
    pallas_call x1, Pallas kernels, body(): pl.pallas_call(kernel, out_shape=[jax.ShapeDtypeStruct((256, 128), jnp.fl...  77.7 us
    unnamed x4, local copies, waits for them, and re-layouts  2.26 us

profile of v1, /device:TPU:1, one launch (start us, length us, event | category | flops | bytes accessed | tf_op | source)
XLA Modules:
  0.0 80.6 jit_solution(11558379818586695079)
XLA Ops:
  0.6 77.7 %shard_map.113 = (f32[256,128]{1,0:T(8,128)}, f32[256,128]{1,0:T(8,128)}) custom-call(f32[256,128]{1,0:T(8,128)} %bitcast.20, f32[256,128]{1,0:T(8,128)} %bitcast.21, f32[256,128]{1,0:T(8,128)} %bitcast.22, f32[256,128]{1,0:T(8,128)} %bitcast.23, bf16[128,128]{1,0:T(8,128)(2,1)} %constant.12.h1h_ref, bf16[128,128]{1,0:T(8,128)(2,1)} %constant.15.h1l_ref, ...), custom_call_target="tpu_custom_call" | custom-call | tf_op jit(solution)/shard_map/pallas_call | solution.py:304
  78.3 0.0 copy-start
  78.3 1.6 %copy.14 = f32[128,16,16]{0,2,1:T(8,128)} copy(f32[128,16,16]{0,2,1:T(8,128)} %bitcast.19) | data formatting | bytes 262144
  79.9 0.0 copy-done
  79.9 0.7 copy.15
Async XLA Ops:
  78.3 1.6 %copy-start = (f32[256,128]{1,0:T(8,128)S(1)}, f32[256,128]{1,0:T(8,128)}, u32[]{:S(2)}) copy-start(f32[256,128]{1,0:T(8,128)} %get-tuple-element.5) | copy-start | bytes 393220

commit v2 on v1

v2 whole, which is shorter than its diff:
```python
import functools

import jax
import jax.numpy as jnp
import numpy as np
from jax import lax
from jax.experimental import pallas as pl
from jax.experimental.pallas import tpu as pltpu
from jax.sharding import PartitionSpec as P

ITERS = 4
NA = 8
NB = 16
ND = NA * NB
MESH = pl.DeviceIdType.MESH
mass_shift = 0.5
base_coef = 1.0


def cas_matrix(points):
    index = np.arange(points)
    angle = 2.0 * np.pi * ((index[:, None] * index[None, :]) % points) / points
    return (np.cos(angle) + np.sin(angle)) / np.sqrt(points)


def split_constant(matrix):
    single = matrix.astype(np.float32)
    high = single.astype(jnp.bfloat16)
    low = (single - high.astype(np.float32)).astype(jnp.bfloat16)
    return high, low


def wave(points):
    return 2.0 - 2.0 * np.cos(2.0 * np.pi * np.arange(points) / points)


def ring_distance(step):
    return min(step, 4 - step)


OFFSETS = [
    (dx, dy, dz, dc)
    for dx in range(4)
    for dy in range(4)
    for dz in range(4)
    for dc in range(2)
    if (dx, dy, dz, dc) != (0, 0, 0, 0)
]
OFFSETS.sort(
    key=lambda o: -(ring_distance(o[0]) + ring_distance(o[1]) + ring_distance(o[2]) + 0.5 * o[3])
)


def split(value):
    high = value.astype(jnp.bfloat16)
    low = (value - high.astype(jnp.float32)).astype(jnp.bfloat16)
    return high, low


def dot(left, right, dims=((1,), (0,))):
    return lax.dot_general(left, right, (dims, ((), ())), preferred_element_type=jnp.float32)


def from_left(stacked, value):
    rows = stacked.shape[0] // 2
    parts = dot(stacked, jnp.concatenate(split(value), axis=0))
    return parts[:rows] + parts[rows:]


def from_right(value, high, low):
    rows = value.shape[0]
    top, bottom = split(value)
    parts = dot(jnp.concatenate([top, bottom], axis=0), high)
    return parts[:rows] + (parts[rows:] + dot(top, low))


def take(buffer, row):
    return buffer.reshape(ND * 4, 128)[pl.ds(row, ND, stride=4), :]


def put(buffer, row, value):
    buffer.reshape(ND * 4, 128)[pl.ds(row, ND, stride=4), :] = value


def lanes_to(value, index):
    return jnp.take_along_axis(value, index, axis=1)


def segment_transpose(value):
    rows = value.shape[0]
    row = lax.broadcasted_iota(jnp.int32, (8, 128), 0)
    lane = lax.broadcasted_iota(jnp.int32, (8, 128), 1)
    group, inner = lane // 16, lane % 16
    first = ((row + group) % 8) * 16 + inner
    middle = (row - group + 8) % 8
    last = ((row - group + 8) % 8) * 16 + inner
    done = []
    for start in range(0, rows, 8):
        tile = value[start : start + 8]
        tile = jnp.take_along_axis(tile, first, axis=1)
        tile = jnp.take_along_axis(tile, middle, axis=0)
        done.append(jnp.take_along_axis(tile, last, axis=1))
    return done


def kernel(
    b_hbm, cx_hbm, cy_hbm, cz_hbm, h1_hbm, h2h_hbm, h2l_hbm, wy_hbm, wz_hbm,
    x_ref, r_ref,
    b_ref, cx_raw, cy_raw, cz_raw, h1_ref, h2h_ref, h2l_ref, wy_ref, wz_ref,
    fs, fr, bs, br, ds, dr, zlast, ylow, zlow,
    cx_ref, cy_ref, cz_ref, lx_ref, ly_ref, lz_ref, diag_ref, inv_ref,
    rhat, shat, u_ref, w_ref, p_ref, s_ref, xs_ref, halo_ref, sc,
    f_send, f_recv, b_send, b_recv, d_send, d_recv, e_sems, in_sems,
):
    loads = [
        pltpu.make_async_copy(source, target, in_sems.at[k])
        for k, (source, target) in enumerate(
            (
                (b_hbm, b_ref), (h1_hbm, h1_ref), (cy_hbm, cy_raw),
                (cz_hbm, cz_raw), (wy_hbm, wy_ref), (wz_hbm, wz_ref), (cx_hbm, cx_raw),
                (h2h_hbm, h2h_ref), (h2l_hbm, h2l_ref),
            )
        )
    ]
    for load in loads:
        load.start()
    a = lax.axis_index("pa")
    b = lax.axis_index("pb")
    me = a * NB + b
    at_y, at_x, core = lax.rem(a, 4), lax.rem(b // 2, 4), lax.rem(b, 2)
    at_z = (b // 8) * 2 + a // 4
    part_x = [lax.rem(at_x + d, 4) * 2 for d in range(4)]
    part_y = [lax.rem(at_y + d, 4) for d in range(4)]
    part_za = [lax.rem(lax.rem(at_z + d, 4), 2) * 4 for d in range(4)]
    part_zb = [(lax.rem(at_z + d, 4) // 2) * 8 for d in range(4)]
    part_c = [core, 1 - core]

    def targets():
        for dx, dy, dz, dc in OFFSETS:
            yield part_za[dz] + part_y[dy], part_zb[dz] + part_x[dx] + part_c[dc]

    def send(source, target, send_sem, recv_sem, ta, tb):
        pltpu.make_async_remote_copy(
            source, target, send_sem, recv_sem, device_id=(ta, tb), device_id_type=MESH
        ).start()

    def exchange(source, target, send_sem, recv_sem):
        for ta, tb in targets():
            send(
                source.at[ta * NB + tb, pl.ds(0, 3)], target.at[me, pl.ds(0, 3)],
                send_sem, recv_sem, ta, tb,
            )
        target[pl.ds(me, 1)] = source[pl.ds(me, 1)]

    def all_others(buffer, sem):
        part = buffer.at[pl.ds(0, ND - 1), pl.ds(0, min(3, buffer.shape[1]))]
        pltpu.make_async_copy(part, part, sem).wait()

    barrier = pltpu.get_barrier_semaphore()
    for ta, tb in targets():
        pl.semaphore_signal(barrier, inc=1, device_id=(ta, tb), device_id_type=MESH)

    for load in loads[:2]:
        load.wait()
    h1 = h1_ref[...]

    def fill(lines, partial):
        put(fs, 0, lines[:, :128])
        put(fs, 1, lines[:, 128:])
        put(fs, 2, jnp.broadcast_to(partial, (ND, 128)))

    fill(from_left(h1, b_ref[...].T), jnp.zeros((1, 128), jnp.float32))
    loads[2].wait()
    loads[3].wait()
    zlast[...] = cz_raw[...].reshape(16, 16, 128)[:, 15, :]
    for ref in (u_ref, w_ref, p_ref, s_ref, xs_ref, rhat, shat):
        ref[...] = jnp.zeros_like(ref)
    sc[...] = jnp.ones_like(sc)

    pl.semaphore_wait(barrier, ND - 1)
    exchange(fs, fr, f_send, f_recv)
    edge_y = pltpu.make_async_remote_copy(
        cy_raw.at[pl.ds(240, 16)], ylow, e_sems.at[0], e_sems.at[1],
        device_id=(lax.rem(a + 1, NA), b), device_id_type=MESH,
    )
    edge_z = pltpu.make_async_remote_copy(
        zlast, zlow, e_sems.at[2], e_sems.at[3],
        device_id=(a, lax.rem(b + 1, NB)), device_id_type=MESH,
    )
    edge_y.start()
    edge_z.start()
    for load in loads[4:]:
        load.wait()

    symbol = mass_shift + base_coef * (
        wy_ref[pl.ds(me, 1), 0:1] + wy_ref[:, 0:1] + wz_ref[...]
    )
    inv_ref[...] = 1.0 / symbol
    cx, cy, cz = cx_raw[...].T, cy_raw[...].T, cz_raw[...].T
    lower_x = pltpu.roll(cx, 1, 0)
    cx_ref[...] = cx
    cy_ref[...] = cy
    cz_ref[...] = cz
    lx_ref[...] = lower_x
    edge_y.wait()
    edge_z.wait()
    lower_y = jnp.concatenate([ylow[...], cy_raw[:240]], axis=0).T
    cube = cz_raw[...].reshape(16, 16, 128)
    lower_z = jnp.concatenate([zlow[...][:, None, :], cube[:, :15]], axis=1).reshape(256, 128).T
    ly_ref[...] = lower_y
    lz_ref[...] = lower_z
    diag_ref[...] = mass_shift + ((cx + lower_x) + (cy + lower_y) + (cz + lower_z))

    lane = lax.broadcasted_iota(jnp.int32, (128, 128), 1)
    in_line = lane % 16
    low_half = jnp.where(
        lane >= 112, lane - 112, jnp.where(lane < 32, (lane % 8) * 16 + 15, (lane % 8) * 16)
    )
    high_half = jnp.where(
        lane < 16, lane + 112, jnp.where(lane < 32, (lane % 8) * 16 + 15, (lane % 8) * 16)
    )
    from_high = (lane < 16) | ((lane < 48) & (in_line >= 8))
    spread = [
        jnp.where(in_line == 0, 16, 32) + half * 8 + lane // 16 for half in range(2)
    ]

    def slab(step, beta):
        tiles = [segment_transpose(take(fr, half)) for half in range(2)]
        plane = jnp.concatenate(
            [
                jnp.concatenate(
                    [tiles[half][2 * row + part] for row in range(NA) for half in range(2)], axis=0
                )
                for part in range(2)
            ],
            axis=1,
        )
        freq = from_right(plane, h2h_ref[...], h2l_ref[...])
        freq = from_left(h1, freq)
        new_s = freq + beta * shat[...]
        new_r = rhat[...] - step * new_s
        shat[...] = new_s
        rhat[...] = new_r
        scaled = new_r * inv_ref[...]
        part_fit = jnp.sum(new_r * scaled, keepdims=True)
        back = from_left(h1, scaled)
        back = from_right(back, h2h_ref[...], h2l_ref[...])
        out = [segment_transpose(back[:, part * 128 : part * 128 + 128]) for part in range(2)]
        halves = [
            jnp.concatenate(
                [out[part][2 * row + half] for row in range(NA) for part in range(2)], axis=0
            )
            for half in range(2)
        ]
        edges = jnp.where(
            from_high, lanes_to(halves[1], high_half), lanes_to(halves[0], low_half)
        )
        cube = edges.reshape(NA, NB, 128)
        from_low_z = jnp.concatenate([cube[:, 15:], cube[:, :15]], axis=1).reshape(ND, 128)
        from_high_z = jnp.concatenate([cube[:, 1:], cube[:, :1]], axis=1).reshape(ND, 128)
        from_low_y = jnp.concatenate([edges[112:], edges[:112]], axis=0)
        from_high_y = jnp.concatenate([edges[16:], edges[:16]], axis=0)
        halo = jnp.where(
            lane < 48,
            jnp.where(lane < 16, from_low_y, jnp.where(lane < 32, from_low_z, from_high_z)),
            jnp.where(lane >= 112, from_high_y, jnp.broadcast_to(part_fit, (ND, 128))),
        )
        put(bs, 0, halves[0])
        put(bs, 1, halves[1])
        put(bs, 2, halo)
        exchange(bs, br, b_send, b_recv)

    def scalars(turn, curvature):
        fit, fit_old, step_old = sc[0:1], sc[1:2], sc[2:3]
        beta = jnp.where(turn <= 1, 0.0, fit / fit_old)
        step = fit / (curvature - jnp.where(turn <= 1, 0.0, beta * fit / step_old))
        return jnp.where(turn == 0, -1.0, step), beta

    def neighbours(u0, u1, halo):
        u = jnp.concatenate([u0, u1], axis=1)
        up = [pltpu.roll(v, 112, 1) for v in (u0, u1)]
        above_y = jnp.concatenate(
            [jnp.where(lane < 112, up[0], up[1]), jnp.where(lane < 112, up[1], halo)], axis=1
        )
        down = [pltpu.roll(v, 16, 1) for v in (u0, u1)]
        below_y = jnp.concatenate(
            [jnp.where(lane >= 16, down[0], halo), jnp.where(lane >= 16, down[1], down[0])], axis=1
        )
        ends = [lanes_to(halo, spread[half]) for half in range(2)]
        above_z = jnp.concatenate(
            [jnp.where(in_line < 15, pltpu.roll(v, 127, 1), e) for v, e in zip((u0, u1), ends)],
            axis=1,
        )
        below_z = jnp.concatenate(
            [jnp.where(in_line > 0, pltpu.roll(v, 1, 1), e) for v, e in zip((u0, u1), ends)],
            axis=1,
        )
        return pltpu.roll(u, 127, 0), pltpu.roll(u, 1, 0), above_y, below_y, above_z, below_z

    def turn_body(turn, carry):
        all_others(fr, f_recv)
        curvature = jnp.sum(take(fr, 2), axis=0, keepdims=True)
        step, beta = scalars(turn, curvature)
        slab(step[:, 0:1], beta[:, 0:1])
        new_p = u_ref[...] + beta[:, 0:1] * p_ref[...]
        new_s = w_ref[...] + beta[:, 0:1] * s_ref[...]
        p_ref[...] = new_p
        s_ref[...] = new_s
        xs_ref[...] = xs_ref[...] + step[:, 0:1] * new_p
        sc[1:2] = sc[0:1]
        sc[2:3] = step

        all_others(br, b_recv)
        total = jnp.sum(take(br, 2), axis=0, keepdims=True)
        sc[0:1] = jnp.broadcast_to(total[:, 64:65], (1, 128))
        u = from_left(h1, jnp.concatenate([take(br, k) for k in range(3)], axis=1))
        u0, u1, halo = u[:, :128], u[:, 128:256], u[:, 256:]
        u = u[:, :256]
        u_ref[...] = u
        above_x, below_x, above_y, below_y, above_z, below_z = neighbours(u0, u1, halo)
        halo_ref[...] = halo
        image = diag_ref[...] * u
        image -= cx_ref[...] * above_x
        image -= lx_ref[...] * below_x
        image -= cy_ref[...] * above_y
        image -= ly_ref[...] * below_y
        image -= cz_ref[...] * above_z
        image -= lz_ref[...] * below_z
        w_ref[...] = image
        partial = jnp.sum(u * image, keepdims=True)
        all_others(fs, f_send)

        @pl.when(turn < ITERS - 1)
        def _():
            fill(from_left(h1, w_ref[...]), partial)
            exchange(fs, fr, f_send, f_recv)

        @pl.when(turn == ITERS - 1)
        def _():
            ds[...] = jnp.broadcast_to(partial, (1, 128))
            for ta, tb in targets():
                send(ds, dr.at[me], d_send, d_recv, ta, tb)
            dr[pl.ds(me, 1)] = ds[...].reshape(1, 1, 128)

        all_others(bs, b_send)
        return carry

    lax.fori_loop(0, ITERS, turn_body, 0)
    beta = (sc[0:1] / sc[1:2])[:, 0:1]
    x_ref[...] = xs_ref[...].T
    u = u_ref[...]
    sides = neighbours(u[:, :128], u[:, 128:], halo_ref[...])
    total = (sides[0] + sides[1]) + (sides[2] + sides[3]) + (sides[4] + sides[5])
    r_ref[...] = ((mass_shift + 6.0 * base_coef) * u - base_coef * total).T
    last_p = (u_ref[...] + beta * p_ref[...]).T
    last_s = (w_ref[...] + beta * s_ref[...]).T
    all_others(dr, d_recv)
    curvature = jnp.sum(dr.reshape(ND, 128)[...], axis=0, keepdims=True)
    step, beta = scalars(ITERS, curvature)
    x_ref[...] = x_ref[...] + step * last_p
    r_ref[...] = r_ref[...] - step * last_s
    all_others(dr, d_send)


def body(right_side, coef_x, coef_y, coef_z):
    def lines(value):
        return value.transpose(1, 2, 0).reshape(256, 128)

    h1 = np.concatenate([np.tile(part, (1, 2)) for part in split_constant(cas_matrix(128))])
    h2 = split_constant(cas_matrix(256))
    wave_y = np.broadcast_to(wave(128)[:, None], (128, 128)).astype(np.float32)
    wave_z = wave(256)[None, :].astype(np.float32)
    args = (
        lines(right_side), lines(coef_x), lines(coef_y), lines(coef_z),
        *(jnp.asarray(v) for v in (h1, h2[0], h2[1], wave_y, wave_z)),
    )
    message = pltpu.VMEM((ND, 4, 128), jnp.float32)
    plane = pltpu.VMEM((128, 256), jnp.float32)
    row = pltpu.VMEM((1, 128), jnp.float32)
    edge = pltpu.VMEM((16, 128), jnp.float32)
    vmem = pl.BlockSpec(memory_space=pltpu.VMEM)
    x, r = pl.pallas_call(
        kernel,
        out_shape=[pltpu.VMEM((256, 128), jnp.float32)] * 2,
        in_specs=[pl.BlockSpec(memory_space=pl.ANY)] * 9,
        out_specs=[vmem] * 2,
        scratch_shapes=[pltpu.VMEM(v.shape, v.dtype) for v in args]
        + [message] * 4 + [row, pltpu.VMEM((ND, 1, 128), jnp.float32)] + [edge] * 3
        + [plane] * 15 + [pltpu.VMEM((128, 128), jnp.float32)] + [pltpu.VMEM((8, 128), jnp.float32)]
        + [pltpu.SemaphoreType.DMA] * 6
        + [pltpu.SemaphoreType.DMA((4,)), pltpu.SemaphoreType.DMA((9,))],
        compiler_params=pltpu.CompilerParams(collective_id=0, has_side_effects=True),
    )(*args)

    def block_of(value):
        return value.reshape(16, 16, 128).transpose(2, 0, 1)

    return block_of(x), block_of(r)


def solution(mesh):
    spec = P(None, "pa", "pb")
    return jax.shard_map(
        body, mesh=mesh, in_specs=(spec,) * 4, out_specs=(spec,) * 2, check_vma=False
    )
```

time: 80.7 us -> 75.4 us (0.934)
  Pallas kernels: 77.7 us -> 73.3 us
  local copies, waits for them, and re-layouts: 2.26 us -> 1.31 us
    pallas_call x1, Pallas kernels: 77.7 us -> 73.3 us  [body(): pl.pallas_call(kernel, out_shape=[pltpu.VMEM((256, 128), jnp.float32)] *...]
    unnamed x4 -> x2, local copies, waits for them, and re-layouts: 2.26 us -> 1.31 us
where the time goes in v2:
time: 75.4 us; the launch traced here: 75.3 us
  Pallas kernels  73.3 us (97%)
  local copies, waits for them, and re-layouts  1.31 us (2%)
    pallas_call x1, Pallas kernels, body(): pl.pallas_call(kernel, out_shape=[pltpu.VMEM((256, 128), jnp.float32)] *...  73.3 us

profile of v2, /device:TPU:1, one launch (start us, length us, event | category | flops | bytes accessed | tf_op | source)
XLA Modules:
  0.0 75.3 jit_solution(5900939181874805500)
XLA Ops:
  0.6 73.3 %shard_map.104 = (f32[256,128]{1,0:T(8,128)S(1)}, f32[256,128]{1,0:T(8,128)S(1)}) custom-call(f32[256,128]{1,0:T(8,128)} %bitcast.20, f32[256,128]{1,0:T(8,128)} %bitcast.21, f32[256,128]{1,0:T(8,128)} %bitcast.22, f32[256,128]{1,0:T(8,128)} %bitcast.23, bf16[256,256]{1,0:T(8,128)(2,1)} %constant.10.clone.h1_hbm, bf16[256,256]{1,0:T(8,128)(2,1)} %constant.11.clone.h2h_hbm, ...), custom_call_target="tpu_custom_call" | custom-call | tf_op jit(solution)/shard_map/pallas_call | solution.py:382
  73.9 0.7 copy.13
  74.6 0.7 copy.14
